TPU v7x, 64 devices: a 2x2x8 block of a 4x4x8 slice. The times are simulated.
64 devices in a mesh: dp: 4 (over x, y), sp: 16 (over z, core).
Axes of the slice: x: 2, y: 2, z: 8, core: 2. Of those that a mesh axis runs over, the one named last changes fastest.
The devices are a block of a 4x4x8 slice.
Arguments:
- signal: bfloat16 [262144, 768], P(('dp', 'sp')), parts along dimension 0
- w_first: bfloat16 [10, 1024, 2, 64, 64], P(None, 'sp')
- w_second: bfloat16 [10, 1024, 2, 64, 64], P(None, 'sp')
Outputs:
- output: bfloat16 [262144, 768], P(('dp', 'sp')), parts along dimension 0
There are 4 independent parts. A program takes and returns all parts, laid end to end along the dimension named above; an argument that names none is the same for every part.
All inputs are finite; a program needn't handle non-finite values.
Results may differ from a plain program's by a relative error of at most 0.02.
Values are sent between devices in bfloat16 or wider.
A program may use at most 768 MiB of HBM per device.

v0:
```python
import jax
import jax.numpy as jnp
from jax import lax
from jax.sharding import PartitionSpec as P


def local_partner(act_blocks, distance):
    num_blocks = act_blocks.shape[0]
    grouped = act_blocks.reshape(num_blocks // (2 * distance), 2, distance, act_blocks.shape[1], act_blocks.shape[2])
    return grouped[:, ::-1].reshape(act_blocks.shape)


def mix_blocks(act_blocks, partner, weights):
    own_part = jnp.einsum("lij,ljc->lic", weights[:, 0], act_blocks, preferred_element_type=jnp.float32)
    cross_part = jnp.einsum("lij,ljc->lic", weights[:, 1], partner, preferred_element_type=jnp.float32)
    return (own_part + cross_part).astype(jnp.bfloat16)


def solution(mesh):
    groups = mesh.shape["sp"]

    def apply_map(act_blocks, weights, distances):
        local_blocks = act_blocks.shape[0]
        for stage, distance in enumerate(distances):
            if distance < local_blocks:
                partner = local_partner(act_blocks, distance)
            else:
                dev_step = distance // local_blocks
                pairing = [(device, device ^ dev_step) for device in range(groups)]
                partner = lax.ppermute(act_blocks, "sp", pairing)
            act_blocks = mix_blocks(act_blocks, partner, weights[stage])
        return act_blocks

    def device_program(signal, w_first, w_second):
        stages = w_first.shape[0]
        local_blocks = w_first.shape[1]
        block_rows = w_first.shape[3]
        act_blocks = signal.reshape(local_blocks, block_rows, signal.shape[1])
        dist_down = [2 ** (stages - 1 - level) for level in range(stages)]
        hidden = apply_map(act_blocks, w_first, dist_down)
        hidden = jax.nn.gelu(hidden.astype(jnp.float32), approximate=False).astype(jnp.bfloat16)
        result = apply_map(hidden, w_second, dist_down[::-1])
        return result.reshape(signal.shape)

    row_spec = P(("dp", "sp"), None)
    weight_spec = P(None, "sp", None, None, None)
    return jax.shard_map(device_program, mesh=mesh, in_specs=(row_spec, weight_spec, weight_spec), out_specs=row_spec, check_vma=False)
```

profile of v0, /device:TPU:84, one launch (start us, length us, event | category | flops | bytes accessed | tf_op | source)
XLA Modules:
  0.0 1729.3 jit_solution(663275769433241611)
XLA Ops:
  6.2 14.6 fusion.54
  26.4 249.8 %collective-permute-done = bf16[64,64,768]{2,1,0:T(8,128)(2,1)} collective-permute-done((bf16[64,64,768]{2,1,0:T(8,128)(2,1)}, bf16[64,64,768]{2,1,0:T(8,128)(2,1)}, u32[]{:S(2)}, u32[]{:S(2)}) %collective-permute-start) | collective-permute-done | bytes 6291488 | tf_op jit(solution)/shard_map/ppermute | solution.py:30
  291.8 261.5 %collective-permute-done.1 = bf16[64,64,768]{2,1,0:T(8,128)(2,1)} collective-permute-done((bf16[64,64,768]{2,1,0:T(8,128)(2,1)}, bf16[64,64,768]{2,1,0:T(8,128)(2,1)}, u32[]{:S(2)}, u32[]{:S(2)}) %collective-permute-start.1) | collective-permute-done | bytes 6291488 | tf_op jit(solution)/shard_map/ppermute | solution.py:30
  553.2 7.6 add_convert_fusion.18
  570.5 127.6 %collective-permute-done.2 = bf16[64,64,768]{2,1,0:T(8,128)(2,1)} collective-permute-done((bf16[64,64,768]{2,1,0:T(8,128)(2,1)}, bf16[64,64,768]{2,1,0:T(8,128)(2,1)}, u32[]{:S(2)}, u32[]{:S(2)}) %collective-permute-start.2) | collective-permute-done | bytes 6291488 | tf_op jit(solution)/shard_map/ppermute | solution.py:30
  698.2 7.6 add_convert_fusion.17
  719.6 15.5 fusion.53
  746.8 7.6 add_convert_fusion.16
  765.4 7.6 add_convert_fusion.15
  821.7 7.6 add_convert_fusion.12
  859.4 30.3 %fusion.2 = bf16[64,64,768]{2,1,0:T(8,128)(2,1)} fusion(f32[64,768,64]{1,2,0:T(8,128)S(1)} %fusion.42, bf16[64,64,768]{2,1,0:T(8,128)(2,1)S(1)} %bitcast.413, bf16[64,2,64,64]{3,2,0,1:T(8,128)(2,1)S(1)} %bitcast.412), kind=kOutput, calls=%fused_computation.5 | convolution fusion | flops 616562688 | bytes 26214400 | tf_op jit(solution)/shard_map/lij,ljc->lic/dot_general | solution.py:15
  900.8 7.6 add_convert_fusion.9
  919.5 7.6 add_convert_fusion.8
  938.2 7.6 add_convert_fusion.7
  957.0 7.6 add_convert_fusion.6
  975.7 7.6 add_convert_fusion.5
  994.3 7.6 add_convert_fusion.4
  1012.5 7.6 add_convert_fusion.3
  1027.8 130.1 %collective-permute-done.5 = bf16[64,64,768]{2,1,0:T(8,128)(2,1)} collective-permute-done((bf16[64,64,768]{2,1,0:T(8,128)(2,1)}, bf16[64,64,768]{2,1,0:T(8,128)(2,1)}, u32[]{:S(2)}, u32[]{:S(2)}) %collective-permute-start.5) | collective-permute-done | bytes 6291488 | tf_op jit(solution)/shard_map/ppermute | solution.py:30
  1157.8 7.6 add_convert_fusion.2
  1176.0 261.8 %collective-permute-done.6 = bf16[64,64,768]{2,1,0:T(8,128)(2,1)} collective-permute-done((bf16[64,64,768]{2,1,0:T(8,128)(2,1)}, bf16[64,64,768]{2,1,0:T(8,128)(2,1)}, u32[]{:S(2)}, u32[]{:S(2)}) %collective-permute-start.6) | collective-permute-done | bytes 6291488 | tf_op jit(solution)/shard_map/ppermute | solution.py:30
  1437.8 7.6 add_convert_fusion.1
  1458.2 263.1 %collective-permute-done.7 = bf16[64,64,768]{2,1,0:T(8,128)(2,1)} collective-permute-done((bf16[64,64,768]{2,1,0:T(8,128)(2,1)}, bf16[64,64,768]{2,1,0:T(8,128)(2,1)}, u32[]{:S(2)}, u32[]{:S(2)}) %collective-permute-start.7) | collective-permute-done | bytes 6291488 | tf_op jit(solution)/shard_map/ppermute | solution.py:30
  1721.3 7.6 add_convert_fusion
  (96 shorter events, 260.2 us)
Async XLA Ops:
  0.0 276.1 %collective-permute-start = (bf16[64,64,768]{2,1,0:T(8,128)(2,1)}, bf16[64,64,768]{2,1,0:T(8,128)(2,1)}, u32[]{:S(2)}, u32[]{:S(2)}) collective-permute-start(bf16[64,64,768]{2,1,0:T(8,128)(2,1)} %bitcast.391), channel_id=1, source_target_pairs={{0,8},{1,9},{2,10},{3,11},{4,12},{5,13},{6,14},{7,15},{8,0},{9,1},... | collective-permute-start | bytes 18874376 | tf_op jit(solution)/shard_map/ppermute | solution.py:30
  21.0 5.4 copy-start.7
  283.7 269.5 %collective-permute-start.1 = (bf16[64,64,768]{2,1,0:T(8,128)(2,1)}, bf16[64,64,768]{2,1,0:T(8,128)(2,1)}, u32[]{:S(2)}, u32[]{:S(2)}) collective-permute-start(bf16[64,64,768]{2,1,0:T(8,128)(2,1)} %add_convert_fusion.19), channel_id=1, source_target_pairs={{0,4},{1,5},{2,6},{3,7},{4,0},{5,1},{6,2},{7,3},{8,12},{9,13},{10,... | collective-permute-start | bytes 18874376 | tf_op jit(solution)/shard_map/ppermute | solution.py:30
  286.4 5.3 copy-start.1
  560.8 137.4 %collective-permute-start.2 = (bf16[64,64,768]{2,1,0:T(8,128)(2,1)}, bf16[64,64,768]{2,1,0:T(8,128)(2,1)}, u32[]{:S(2)}, u32[]{:S(2)}) collective-permute-start(bf16[64,64,768]{2,1,0:T(8,128)(2,1)} %bitcast.376), channel_id=1, source_target_pairs={{0,2},{1,3},{2,0},{3,1},{4,6},{5,7},{6,4},{7,5},{8,10},{9,11},{10,... | collective-permute-start | bytes 18874376 | tf_op jit(solution)/shard_map/ppermute | solution.py:30
  565.2 5.3 copy-start.2
  705.8 6.4 copy-start.8
  705.8 41.0 %collective-permute-start.3 = (bf16[64,64,768]{2,1,0:T(8,128)(2,1)}, bf16[64,64,768]{2,1,0:T(8,128)(2,1)}, u32[]{:S(2)}, u32[]{:S(2)}) collective-permute-start(bf16[64,64,768]{2,1,0:T(8,128)(2,1)} %bitcast.372), channel_id=1, source_target_pairs={{0,1},{1,0},{2,3},{3,2},{4,5},{5,4},{6,7},{7,6},{8,9},{9,8},{10,11... | collective-permute-start | bytes 18874376 | tf_op jit(solution)/shard_map/ppermute | solution.py:30
  705.8 7.9 copy-start.11
  705.8 7.9 copy-start.12
  712.2 4.4 copy-start.9
  712.2 4.4 copy-start.10
  738.4 6.6 slice-start
  741.7 3.3 slice-start.1
  848.4 6.3 copy-start.13
  854.7 4.7 copy-start.14
  1002.0 10.5 collective-permute-start.4
  1004.4 5.3 copy-start.3
  1020.1 137.7 %collective-permute-start.5 = (bf16[64,64,768]{2,1,0:T(8,128)(2,1)}, bf16[64,64,768]{2,1,0:T(8,128)(2,1)}, u32[]{:S(2)}, u32[]{:S(2)}) collective-permute-start(bf16[64,64,768]{2,1,0:T(8,128)(2,1)} %bitcast.378), channel_id=1, source_target_pairs={{0,2},{1,3},{2,0},{3,1},{4,6},{5,7},{6,4},{7,5},{8,10},{9,11},{10,... | collective-permute-start | bytes 18874376 | tf_op jit(solution)/shard_map/ppermute | solution.py:30
  1022.4 5.3 copy-start.4
  1165.4 272.4 %collective-permute-start.6 = (bf16[64,64,768]{2,1,0:T(8,128)(2,1)}, bf16[64,64,768]{2,1,0:T(8,128)(2,1)}, u32[]{:S(2)}, u32[]{:S(2)}) collective-permute-start(bf16[64,64,768]{2,1,0:T(8,128)(2,1)} %bitcast.379), channel_id=1, source_target_pairs={{0,4},{1,5},{2,6},{3,7},{4,0},{5,1},{6,2},{7,3},{8,12},{9,13},{10,... | collective-permute-start | bytes 18874376 | tf_op jit(solution)/shard_map/ppermute | solution.py:30
  1170.7 5.3 copy-start.5
  1445.5 275.8 %collective-permute-start.7 = (bf16[64,64,768]{2,1,0:T(8,128)(2,1)}, bf16[64,64,768]{2,1,0:T(8,128)(2,1)}, u32[]{:S(2)}, u32[]{:S(2)}) collective-permute-start(bf16[64,64,768]{2,1,0:T(8,128)(2,1)} %bitcast.375), channel_id=1, source_target_pairs={{0,8},{1,9},{2,10},{3,11},{4,12},{5,13},{6,14},{7,15},{8,0},{9,1},... | collective-permute-start | bytes 18874376 | tf_op jit(solution)/shard_map/ppermute | solution.py:30
  1452.9 5.4 copy-start.6
  (1 other events, 3.3 us)
where the time goes:
time: 1740 us; the launch traced here: 1730 us
  waiting for transfers between devices  1300 us (75%)
  matrix products  273 us (16%)
  local copies, waits for them, and re-layouts  139 us (8%)
  starting transfers between devices  20.1 us (1%)
    ppermute x8, waiting for transfers between devices, apply_map(): partner = lax.ppermute(act_blocks, 'sp', pairing)  1300 us
    dot_general x20, matrix products, mix_blocks(): jnp.einsum('lij,ljc->lic', weights[:, 1], partner, preferred_element_type...  175 us
    dot_general x20, matrix products, mix_blocks(): jnp.einsum('lij,ljc->lic', weights[:, 0], act_blocks, preferred_element_t...  98.3 us
    rev x12, local copies, waits for them, and re-layouts, local_partner(): return grouped[:, ::-1].reshape(act_blocks.shape)  74.3 us
  transfers between devices with their start and end apart: 8, of which 7 were waited for; matrix products, arithmetic and copies ran while one was open for 6% of the time, Pallas kernels for 0%

commit v1 on v0

v1 whole, which is shorter than its diff:
```python
import functools
import math

import jax
import jax.numpy as jnp
from jax import lax
from jax.experimental import pallas as pl
from jax.experimental.pallas import tpu as pltpu
from jax.sharding import PartitionSpec as P

MESH = pl.DeviceIdType.MESH
BF16 = jnp.bfloat16
F32 = jnp.float32
CHUNK = 256
UNROLL = 8


def gelu(x):
    return 0.5 * x * (1.0 + lax.erf(x * (0.5 ** 0.5)))


def mix_stage(src, dst, weights, stage, step, act):
    pairs = src.shape[0] // 2
    unroll = min(UNROLL, pairs)

    @pl.loop(0, pairs // unroll)
    def _(it):
        for u in range(unroll):
            p = it * unroll + u
            i = (p // step) * (2 * step) + p % step
            j = i + step
            z = jnp.concatenate([src[i], src[j]], axis=0)
            w = jnp.concatenate([weights(stage, i), weights(stage, j)], axis=0)
            o = jnp.dot(w, z, preferred_element_type=F32).astype(BF16)
            if act:
                o = gelu(o.astype(F32)).astype(BF16)
            half = o.shape[0] // 2
            dst[i] = o[:half]
            dst[j] = o[half:]


def run_stages(buf, tmp, plan):
    src, dst = buf, tmp
    for weights, stage, step, act in plan:
        mix_stage(src, dst, weights, stage, step, act)
        src, dst = dst, src
    return src


def kernel(n, groups, sub, x, wa, wb, out, r1, r2, r3, tmp, ta, tb, la, lb,
           x_snd, x_rcv, o1_snd, o1_rcv, i2_snd, i2_rcv, o2_snd, o2_rcv,
           z_snd, z_rcv, g_snd, g_rcv, l_sem):
    me = lax.axis_index("sp")
    dp = lax.axis_index("dp")
    my_part = dp % sub
    base = dp - my_part
    chunks, blocks = r1.shape[0], r1.shape[1]
    per = blocks // n
    cross = int(math.log2(n))
    local = wa.shape[0] - cross
    items = cross * per // sub
    unit = min(items, per)
    units = items // unit

    def peer(t):
        side = 1 - 2 * (t % 2)
        return (me + n // 2 + side * ((t + 1) // 2) + n) % n

    barrier = pltpu.get_barrier_semaphore()

    @pl.loop(0, n - 1)
    def _(t):
        pl.semaphore_signal(barrier, inc=1, device_id={"sp": peer(t)}, device_id_type=MESH)

    for k in range(1, sub):
        pl.semaphore_signal(barrier, inc=1, device_id={"dp": base + (my_part + k) % sub}, device_id_type=MESH)
    pl.semaphore_wait(barrier, n - 1 + sub - 1)

    def cols(c):
        return pl.ds(pl.multiple_of(c * CHUNK, CHUNK), CHUNK)

    def mine(d):
        return pl.ds(d * per, per)

    def item_of(part, q):
        first = part * items + q * unit
        return first // per, first % per

    def send_weights(m, w, first_stage, t_buf):
        for q in range(units):
            s, l0 = item_of(my_part, q)

            @pl.loop(0, n - 1)
            def _(t):
                d = peer(t)
                pltpu.make_async_remote_copy(
                    src_ref=w.at[first_stage + s, pl.ds(d * per + l0, unit)],
                    dst_ref=t_buf.at[s, me, pl.ds(l0, unit)],
                    send_sem=z_snd.at[m, q], recv_sem=z_rcv.at[m, q],
                    device_id={"sp": d}, device_id_type=MESH).start()

            pltpu.make_async_copy(
                w.at[first_stage + s, pl.ds(me * per + l0, unit)],
                t_buf.at[s, me, pl.ds(l0, unit)], z_rcv.at[m, q]).start()

    def part_ref(t_buf, part, q):
        s, l0 = item_of(part, q)
        return t_buf.at[s, :, pl.ds(l0, unit)]

    def gather_copy(m, t_buf, k, q):
        mine_ref = part_ref(t_buf, my_part, q)
        return pltpu.make_async_remote_copy(
            src_ref=mine_ref, dst_ref=mine_ref,
            send_sem=g_snd.at[m, k, q], recv_sem=g_rcv.at[m, k, q],
            device_id={"dp": base + (my_part + k) % sub}, device_id_type=MESH)

    def start_gather(m, t_buf):
        for q in range(units):
            ref = part_ref(t_buf, my_part, q)
            pltpu.make_async_copy(ref, ref, z_rcv.at[m, q]).wait()
        for k in range(1, sub):
            for q in range(units):
                gather_copy(m, t_buf, k, q).start()

    def wait_gather(m, t_buf):
        for k in range(1, sub):
            for q in range(units):
                ref = part_ref(t_buf, (my_part - k + sub) % sub, q)
                pltpu.make_async_copy(ref, ref, g_rcv.at[m, k, q]).wait()

    send_weights(0, wa, 0, ta)

    @pl.loop(0, chunks)
    def _(c):
        @pl.loop(0, n - 1)
        def _(t):
            d = peer(t)
            pltpu.make_async_remote_copy(
                src_ref=x.at[mine(d), :, cols(c)], dst_ref=r1.at[c, mine(me)],
                send_sem=x_snd.at[c], recv_sem=x_rcv.at[c],
                device_id={"sp": d}, device_id_type=MESH).start()

        pltpu.make_async_copy(x.at[mine(me), :, cols(c)], r1.at[c, mine(me)], x_rcv.at[c]).start()

    send_weights(1, wb, local, tb)
    load_a = pltpu.make_async_copy(wa.at[pl.ds(cross, local)], la, l_sem.at[0])
    load_b = pltpu.make_async_copy(wb.at[pl.ds(0, local)], lb, l_sem.at[1])
    load_a.start()
    load_b.start()

    start_gather(0, ta)
    wait_gather(0, ta)

    def exchanged(t_buf):
        return lambda s, i: t_buf[s, i // per, i % per]

    def kept(l_buf):
        return lambda s, i: l_buf[s, i]

    cross_steps = [per * 2 ** s for s in range(cross)]
    local_steps = [2 ** s for s in range(local)]
    plan_t1 = [(exchanged(ta), s, step, False) for s, step in enumerate(cross_steps[::-1])]
    plan_n = [(kept(la), s, step, step == 1) for s, step in enumerate(local_steps[::-1])]
    plan_n += [(kept(lb), s, step, False) for s, step in enumerate(local_steps)]
    plan_t2 = [(exchanged(tb), s, step, False) for s, step in enumerate(cross_steps)]

    def exchange(src, dst, c, snd, rcv):
        @pl.loop(0, n - 1)
        def _(t):
            d = peer(t)
            pltpu.make_async_remote_copy(
                src_ref=src.at[c, mine(d)], dst_ref=dst.at[c, mine(me)],
                send_sem=snd.at[c], recv_sem=rcv.at[c],
                device_id={"sp": d}, device_id_type=MESH).start()

        dst[c, mine(me)] = src[c, mine(me)]

    def others(ref, c):
        return ref.at[c, pl.ds(0, (n - 1) * per)]

    def wait_for(ref, sem):
        pltpu.make_async_copy(ref, ref, sem).wait()

    @pl.loop(0, chunks)
    def _(c):
        wait_for(r1.at[c], x_rcv.at[c])
        run_stages(r1.at[c], tmp, plan_t1)
        exchange(r1, r2, c, o1_snd, o1_rcv)

    start_gather(1, tb)
    load_a.wait()
    load_b.wait()

    @pl.loop(0, chunks)
    def _(c):
        wait_for(others(r2, c), o1_rcv.at[c])
        run_stages(r2.at[c], tmp, plan_n)
        exchange(r2, r3, c, i2_snd, i2_rcv)

    wait_gather(1, tb)

    @pl.loop(0, chunks)
    def _(c):
        wait_for(others(r3, c), i2_rcv.at[c])
        run_stages(r3.at[c], tmp, plan_t2)

        @pl.loop(0, n - 1)
        def _(t):
            d = peer(t)
            pltpu.make_async_remote_copy(
                src_ref=r3.at[c, mine(d)], dst_ref=out.at[mine(me), :, cols(c)],
                send_sem=o2_snd.at[c], recv_sem=o2_rcv.at[c],
                device_id={"sp": d}, device_id_type=MESH).start()

        pltpu.make_async_copy(r3.at[c, mine(me)], out.at[mine(me), :, cols(c)], o2_rcv.at[c]).start()

    @pl.loop(0, chunks)
    def _(c):
        wait_for(others(r1, c), x_snd.at[c])
        wait_for(others(r1, c), o1_snd.at[c])
        wait_for(others(r2, c), i2_snd.at[c])
        wait_for(others(r3, c), o2_snd.at[c])
        wait_for(out.at[:, :, cols(c)], o2_rcv.at[c])

    for m, t_buf in enumerate((ta, tb)):
        for q in range(units):
            s, l0 = item_of(my_part, q)
            wait_for(t_buf.at[s, pl.ds(0, n - 1), pl.ds(l0, unit)], z_snd.at[m, q])
            for k in range(1, sub):
                gather_copy(m, t_buf, k, q).wait_send()


def solution(mesh):
    n = mesh.shape["sp"]
    groups = mesh.shape["dp"]

    def pair_weights(w, distances):
        blocks = w.shape[1]
        index = lax.axis_index("sp") * blocks + jnp.arange(blocks)
        upper = jnp.stack([(index // d) % 2 for d in distances]) == 1
        own, cross = w[:, :, 0], w[:, :, 1]
        upper = upper[:, :, None, None]
        return jnp.concatenate([jnp.where(upper, cross, own), jnp.where(upper, own, cross)], axis=-1)

    def device_program(signal, w_first, w_second):
        stages, blocks, rows = w_first.shape[0], w_first.shape[1], w_first.shape[3]
        channels = signal.shape[1]
        chunks = channels // CHUNK
        cross = int(math.log2(n))
        local = stages - cross
        per = blocks // n
        sub = math.gcd(groups, cross * per)
        items = cross * per // sub
        units = items // min(items, per)
        down = [2 ** (stages - 1 - level) for level in range(stages)]
        wa = pair_weights(w_first, down)
        wb = pair_weights(w_second, down[::-1])
        x = signal.reshape(blocks, rows, channels)
        dma = pltpu.SemaphoreType.DMA
        buffer = pltpu.VMEM((chunks, blocks, rows, CHUNK), BF16)
        result = pl.pallas_call(
            functools.partial(kernel, n, groups, sub),
            out_shape=jax.ShapeDtypeStruct(x.shape, BF16),
            in_specs=[pl.BlockSpec(memory_space=pl.ANY)] * 3,
            out_specs=pl.BlockSpec(memory_space=pl.ANY),
            scratch_shapes=[
                buffer, buffer, buffer,
                pltpu.VMEM((blocks, rows, CHUNK), BF16),
                pltpu.VMEM((cross, n, per, rows, 2 * rows), BF16),
                pltpu.VMEM((cross, n, per, rows, 2 * rows), BF16),
                pltpu.VMEM((local, blocks, rows, 2 * rows), BF16),
                pltpu.VMEM((local, blocks, rows, 2 * rows), BF16),
                dma((chunks,)), dma((chunks,)), dma((chunks,)), dma((chunks,)),
                dma((chunks,)), dma((chunks,)), dma((chunks,)), dma((chunks,)),
                dma((2, units)), dma((2, units)), dma((2, sub, units)), dma((2, sub, units)),
                dma((2,)),
            ],
            compiler_params=pltpu.CompilerParams(
                collective_id=0, has_side_effects=True, vmem_limit_bytes=60 * 2 ** 20),
        )(x, wa, wb)
        return result.reshape(signal.shape)

    row_spec = P(("dp", "sp"), None)
    weight_spec = P(None, "sp", None, None, None)
    return jax.shard_map(device_program, mesh=mesh, in_specs=(row_spec, weight_spec, weight_spec), out_specs=row_spec, check_vma=False)
```

time: 1740 us -> 645 us (0.37)
  waiting for transfers between devices: 1300 us -> 0 us
  Pallas kernels: 0 us -> 602 us
  matrix products: 273 us -> 0 us
  local copies, waits for them, and re-layouts: 139 us -> 5.99 us
  other arithmetic: 0.01 us -> 31.7 us
  starting transfers between devices: 20.1 us -> 0 us
    ppermute x8 -> x0, waiting for transfers between devices: 1300 us -> none  [apply_map(): partner = lax.ppermute(act_blocks, 'sp', pairing)]
    pallas_call x0 -> x1, Pallas kernels: none -> 602 us  [device_program(): pl.pallas_call(functools.partial(kernel, n, groups, sub), out_shape=jax.S...]
    dot_general x40 -> x0, matrix products: 273 us -> none  [the longest x20 175 us: mix_blocks(): jnp.einsum('lij,ljc->lic', weights[:, 1], partner, preferred_element_type...]
    rev x12 -> x0, local copies, waits for them, and re-layouts: 74.3 us -> none  [local_partner(): return grouped[:, ::-1].reshape(act_blocks.shape)]
    slice x2 -> x0, local copies, waits for them, and re-layouts: 30.1 us -> none  [apply_map(): act_blocks = mix_blocks(act_blocks, partner, weights[stage])]
    ppermute x8 -> x0, starting transfers between devices: 20.1 us -> none  [apply_map(): partner = lax.ppermute(act_blocks, 'sp', pairing)]
  transfers between devices with their start and end apart: 8 -> 0, of which waited for: 7 -> 0; matrix products, arithmetic and copies ran while one was open for 6% -> 0% of each run, Pallas kernels for 0% -> 0%
where the time goes in v1:
time: 645 us; the launch traced here: 640 us
  Pallas kernels  602 us (93%)
  other arithmetic  31.7 us (5%)
    pallas_call x1, Pallas kernels, device_program(): pl.pallas_call(functools.partial(kernel, n, groups, sub), out_shape=jax.S...  602 us
    select_n x2, other arithmetic, pair_weights(): jnp.where(upper, cross, own)  16.4 us
    concatenate x2, other arithmetic, pair_weights(): jnp.concatenate([jnp.where(upper, cross, own), jnp.where(upper, own, cros...  15.1 us

profile of v1, /device:TPU:84, one launch (start us, length us, event | category | flops | bytes accessed | tf_op | source)
XLA Modules:
  0.0 639.7 jit_solution(2812905409666203754)
XLA Ops:
  0.2 8.2 %bitcast_select_fusion.3 = (bf16[10,64,64,64]{3,2,1,0:T(8,128)(2,1)S(1)}, bf16[10,64,64,64]{3,2,1,0:T(8,128)(2,1)S(1)}) fusion(pred[10,64]{1,0:T(8,128)(4,1)S(1)} %broadcast_compare_fusion.1, bf16[10,64,2,64,64]{4,3,2,1,0:T(8,128)(2,1)} %param.4), kind=kLoop, calls=%fused_computation.5 | loop fusion | flops 5242880 | bytes 20972160 | tf_op jit(solution)/shard_map/jit(_where)/select_n | solution.py:243
  8.5 7.6 %pad_maximum_fusion.wa = bf16[10,64,64,128]{3,2,1,0:T(8,128)(2,1)} fusion(bf16[10,64,64,64]{3,2,1,0:T(8,128)(2,1)S(1)} %get-tuple-element.8, bf16[10,64,64,64]{3,2,1,0:T(8,128)(2,1)S(1)} %get-tuple-element.7), kind=kLoop, calls=%fused_computation | loop fusion | flops 20971520 | bytes 20971520 | tf_op jit(solution)/shard_map/concatenate | solution.py:243
  16.1 8.2 %bitcast_select_fusion.1 = (bf16[10,64,64,64]{3,2,1,0:T(8,128)(2,1)S(1)}, bf16[10,64,64,64]{3,2,1,0:T(8,128)(2,1)S(1)}) fusion(pred[10,64]{1,0:T(8,128)(4,1)S(1)} %broadcast_compare_fusion, bf16[10,64,2,64,64]{4,3,2,1,0:T(8,128)(2,1)} %param.5), kind=kLoop, calls=%fused_computation.3 | loop fusion | flops 5242880 | bytes 20972160 | tf_op jit(solution)/shard_map/jit(_where)/select_n | solution.py:243
  24.3 7.5 %pad_maximum_fusion.1.wb = bf16[10,64,64,128]{3,2,1,0:T(8,128)(2,1)} fusion(bf16[10,64,64,64]{3,2,1,0:T(8,128)(2,1)S(1)} %get-tuple-element.6, bf16[10,64,64,64]{3,2,1,0:T(8,128)(2,1)S(1)} %get-tuple-element.5), kind=kLoop, calls=%fused_computation.1 | loop fusion | flops 20971520 | bytes 20971520 | tf_op jit(solution)/shard_map/concatenate | solution.py:243
  31.8 602.0 %shard_map.37 = bf16[64,64,768]{2,1,0:T(8,128)(2,1)} custom-call(bf16[64,64,768]{2,1,0:T(8,128)(2,1)} %bitcast.23, bf16[10,64,64,128]{3,2,1,0:T(8,128)(2,1)} %pad_maximum_fusion.wa, bf16[10,64,64,128]{3,2,1,0:T(8,128)(2,1)} %pad_maximum_fusion.1.wb), custom_call_target="tpu_custom_call" | custom-call | tf_op jit(solution)/shard_map/pallas_call | solution.py:261
  633.8 5.9 copy.13
  (9 shorter events, 0.2 us)

commit v2 on v0

v2 whole, which is shorter than its diff:
```python
import functools
import math

import jax
import jax.numpy as jnp
from jax import lax
from jax.experimental import pallas as pl
from jax.experimental.pallas import tpu as pltpu
from jax.sharding import PartitionSpec as P

MESH = pl.DeviceIdType.MESH
BF16 = jnp.bfloat16
F32 = jnp.float32
CHUNK = 256
UNROLL = 8
CORES = 2


def gelu(x):
    return 0.5 * x * (1.0 + lax.erf(x * (0.5 ** 0.5)))


def mix_stage(src, dst, weights, step, act):
    pairs = src.shape[0] // 2
    unroll = min(UNROLL, pairs)

    @pl.loop(0, pairs // unroll)
    def _(it):
        for u in range(unroll):
            p = it * unroll + u
            i = (p // step) * (2 * step) + p % step
            j = i + step
            z = jnp.concatenate([src[i], src[j]], axis=0)
            w = jnp.concatenate([weights(i), weights(j)], axis=0)
            o = jnp.dot(w, z, preferred_element_type=F32).astype(BF16)
            if act:
                o = gelu(o.astype(F32)).astype(BF16)
            half = o.shape[0] // 2
            dst[i] = o[:half]
            dst[j] = o[half:]


def partner_stage(own, other, dst, weights):
    blocks = own.shape[0]
    unroll = min(UNROLL, blocks)

    @pl.loop(0, blocks // unroll)
    def _(it):
        for u in range(unroll):
            i = it * unroll + u
            z = jnp.concatenate([own[i], other[i]], axis=0)
            dst[i] = jnp.dot(weights(i), z, preferred_element_type=F32).astype(BF16)


def kernel(n, sub, x, wa, wb, out, r1, r2, r3, rp, tmp, tmq, ta, tb, la, lb, wz, raw,
           x_snd, x_rcv, o1_snd, o1_rcv, i2_snd, i2_rcv, o2_snd, o2_rcv, p_snd, p_rcv,
           z_snd, z_rcv, g_snd, g_rcv, raw_sem):
    me = lax.axis_index("sp")
    dp = lax.axis_index("dp")
    chip, core = me // CORES, me % CORES
    partner = {"sp": me + 1 - 2 * core}
    part = dp % sub
    base = dp - part
    chunks, blocks = r1.shape[0], r1.shape[1]
    stages = wa.shape[0]
    chips = n // CORES
    far = ta.shape[0]
    near = stages - far
    per = blocks // chips
    take = per // sub
    mine_l = pl.ds(part * take, take)

    def peer(t):
        side = 1 - 2 * (t % 2)
        return (chip + chips // 2 + side * ((t + 1) // 2) + chips) % chips

    def on(z):
        return {"sp": z * CORES + core}

    def group(k):
        return {"dp": base + (part + k) % sub}

    def cols(c):
        return pl.ds(pl.multiple_of(c * CHUNK, CHUNK), CHUNK)

    def of(z):
        return pl.ds(z * per, per)

    def wait_for(ref, sem):
        pltpu.make_async_copy(ref, ref, sem).wait()

    barrier = pltpu.get_barrier_semaphore()

    @pl.loop(0, chips - 1)
    def _(t):
        pl.semaphore_signal(barrier, inc=1, device_id=on(peer(t)), device_id_type=MESH)

    pl.semaphore_signal(barrier, inc=1, device_id=partner, device_id_type=MESH)
    for k in range(1, sub):
        pl.semaphore_signal(barrier, inc=1, device_id=group(k), device_id_type=MESH)
    pl.semaphore_wait(barrier, chips + sub - 1)

    jobs = [(m, s, True) for m in range(2) for s in range(far)]
    jobs += [(m, s, False) for m in range(2) for s in range(near)]
    w_of, t_of, l_of = (wa, wb), (ta, tb), (la, lb)

    def load(job):
        m, s, is_far = jobs[job]
        slot = job % 2
        if is_far:
            src = w_of[m].at[(0, near)[m] + s, :, mine_l]
            dst = raw.at[slot, :, pl.ds(0, take)]
        else:
            src, dst = w_of[m].at[(far, 0)[m] + s], raw.at[slot]
        return pltpu.make_async_copy(src, dst, raw_sem.at[slot])

    def prepare(job):
        m, s, is_far = jobs[job]
        slot = job % 2
        if is_far:
            upper = (chip // 2 ** (far - 1 - s, s)[m]) % 2 == 1

            @pl.loop(0, chips)
            def _(z):
                for b in range(take):
                    own, cross = raw[slot, z, b, 0], raw[slot, z, b, 1]
                    left, right = jnp.where(upper, cross, own), jnp.where(upper, own, cross)
                    wz[m, s, z, b] = jnp.concatenate([left, right], axis=-1)
        else:
            level = (near - 1 - s, s)[m]
            step = 2 ** level

            @pl.loop(0, blocks // 8)
            def _(it):
                for u in range(4):
                    p = it * 4 + u
                    i = (p // step) * (2 * step) + p % step
                    j = i + step
                    if level == near - 1:
                        i, j, swap = 2 * p, 2 * p + 1, False
                    else:
                        swap = True
                    first = [raw[slot, i // per, i % per, h] for h in range(2)]
                    second = [raw[slot, j // per, j % per, h] for h in range(2)]
                    l_of[m][s, i] = jnp.concatenate(first, axis=-1)
                    l_of[m][s, j] = jnp.concatenate(second[::-1] if swap else second, axis=-1)

    def run_jobs(first, last):
        for job in range(first, last):
            load(job).wait()
            prepare(job)
            if job + 2 < len(jobs):
                load(job + 2).start()

    def send_weights(m):
        @pl.loop(0, chips - 1)
        def _(t):
            z = peer(t)
            pltpu.make_async_remote_copy(
                src_ref=wz.at[m, :, z], dst_ref=t_of[m].at[:, chip, mine_l],
                send_sem=z_snd.at[m], recv_sem=z_rcv.at[m],
                device_id=on(z), device_id_type=MESH).start()

        for s in range(far):
            for b in range(take):
                t_of[m][s, chip, part * take + b] = wz[m, s, chip, b]

    def gather_copy(m, k):
        ref = t_of[m].at[:, :, mine_l]
        return pltpu.make_async_remote_copy(
            src_ref=ref, dst_ref=ref, send_sem=g_snd.at[m, k], recv_sem=g_rcv.at[m, k],
            device_id=group(k), device_id_type=MESH)

    def start_gather(m):
        wait_for(t_of[m].at[:, pl.ds(0, chips - 1), mine_l], z_rcv.at[m])
        for k in range(1, sub):
            gather_copy(m, k).start()

    def wait_gather(m):
        for k in range(1, sub):
            theirs = (part - k + sub) % sub
            wait_for(t_of[m].at[:, :, pl.ds(theirs * take, take)], g_rcv.at[m, k])

    def send_signal(c):
        @pl.loop(0, chips - 1)
        def _(t):
            z = peer(t)
            pltpu.make_async_remote_copy(
                src_ref=x.at[of(z), :, cols(c)], dst_ref=r1.at[c, of(chip)],
                send_sem=x_snd.at[c], recv_sem=x_rcv.at[c],
                device_id=on(z), device_id_type=MESH).start()

        pltpu.make_async_copy(x.at[of(chip), :, cols(c)], r1.at[c, of(chip)], x_rcv.at[c]).start()

    load(0).start()
    load(1).start()
    send_signal(0)
    run_jobs(0, far)
    send_weights(0)

    @pl.loop(1, chunks)
    def _(c):
        send_signal(c)

    run_jobs(far, 2 * far)
    send_weights(1)
    run_jobs(2 * far, len(jobs))
    start_gather(0)
    wait_gather(0)

    def far_weights(m, s):
        return lambda i: t_of[m][s, i // per, i % per]

    def near_weights(m, s):
        return lambda i: l_of[m][s, i]

    far_steps = [per * 2 ** s for s in range(far)]
    plan_t1 = [(far_weights(0, s), step, False) for s, step in enumerate(far_steps[::-1])]
    plan_t2 = [(far_weights(1, s), step, False) for s, step in enumerate(far_steps)]
    near_steps = [2 ** s for s in range(near - 1)]
    plan_n = [(near_weights(0, s + 1), step, step == 1) for s, step in enumerate(near_steps[::-1])]
    plan_n += [(near_weights(1, s), step, False) for s, step in enumerate(near_steps)]

    def run_far(buf, plan):
        src = buf
        for k, (weights, step, act) in enumerate(plan):
            dst = buf if k == len(plan) - 1 else (tmp, tmq)[k % 2]
            mix_stage(src, dst, weights, step, act)
            src = dst

    def others(ref, c):
        return ref.at[c, pl.ds(0, (chips - 1) * per)]

    def exchange(src, dst, c, snd, rcv):
        @pl.loop(0, chips - 1)
        def _(t):
            z = peer(t)
            pltpu.make_async_remote_copy(
                src_ref=src.at[c, of(z)], dst_ref=dst.at[c, of(chip)],
                send_sem=snd.at[c], recv_sem=rcv.at[c],
                device_id=on(z), device_id_type=MESH).start()

        dst[c, of(chip)] = src[c, of(chip)]

    @pl.loop(0, chunks)
    def _(c):
        wait_for(r1.at[c], x_rcv.at[c])
        run_far(r1.at[c], plan_t1)
        exchange(r1, r2, c, o1_snd, o1_rcv)

    start_gather(1)

    def partner_copy(k, src, dst, c):
        return pltpu.make_async_remote_copy(
            src_ref=src, dst_ref=dst, send_sem=p_snd.at[k, c], recv_sem=p_rcv.at[k, c],
            device_id=partner, device_id_type=MESH)

    @pl.loop(0, chunks)
    def _(c):
        wait_for(others(r2, c), o1_rcv.at[c])
        wait_for(others(r1, c), o1_snd.at[c])
        copy = partner_copy(0, r2.at[c], rp.at[c], c)
        copy.start()
        copy.wait_recv()
        partner_stage(r2.at[c], rp.at[c], tmp, near_weights(0, 0))
        copy.wait_send()
        src, dst = tmp, r2.at[c]
        for weights, step, act in plan_n:
            mix_stage(src, dst, weights, step, act)
            src, dst = dst, src
        copy = partner_copy(1, tmp, r1.at[c], c)
        copy.start()
        copy.wait_recv()
        partner_stage(tmp, r1.at[c], r2.at[c], near_weights(1, near - 1))
        copy.wait_send()
        exchange(r2, r3, c, i2_snd, i2_rcv)

    wait_gather(1)

    @pl.loop(0, chunks)
    def _(c):
        wait_for(others(r3, c), i2_rcv.at[c])
        run_far(r3.at[c], plan_t2)

        @pl.loop(0, chips - 1)
        def _(t):
            z = peer(t)
            pltpu.make_async_remote_copy(
                src_ref=r3.at[c, of(z)], dst_ref=out.at[of(chip), :, cols(c)],
                send_sem=o2_snd.at[c], recv_sem=o2_rcv.at[c],
                device_id=on(z), device_id_type=MESH).start()

        pltpu.make_async_copy(r3.at[c, of(chip)], out.at[of(chip), :, cols(c)], o2_rcv.at[c]).start()

    for m in range(2):
        wait_for(t_of[m].at[:, pl.ds(0, chips - 1), mine_l], z_snd.at[m])
        for k in range(1, sub):
            gather_copy(m, k).wait_send()

    @pl.loop(0, chunks)
    def _(c):
        wait_for(others(r1, c), x_snd.at[c])
        wait_for(others(r2, c), i2_snd.at[c])
        wait_for(others(r3, c), o2_snd.at[c])
        wait_for(out.at[:, :, cols(c)], o2_rcv.at[c])


def solution(mesh):
    n = mesh.shape["sp"]
    groups = mesh.shape["dp"]
    chips = n // CORES
    far = int(math.log2(chips))

    def device_program(signal, w_first, w_second):
        stages, blocks, _, rows, _ = w_first.shape
        channels = signal.shape[1]
        chunks = channels // CHUNK
        near = stages - far
        per = blocks // chips
        sub = math.gcd(groups, per)
        x = signal.reshape(blocks, rows, channels)
        by_chip = (stages, chips, per, 2, rows, rows)
        dma = pltpu.SemaphoreType.DMA
        buffer = pltpu.VMEM((chunks, blocks, rows, CHUNK), BF16)
        temp = pltpu.VMEM((blocks, rows, CHUNK), BF16)
        far_w = pltpu.VMEM((far, chips, per, rows, 2 * rows), BF16)
        near_w = pltpu.VMEM((near, blocks, rows, 2 * rows), BF16)
        result = pl.pallas_call(
            functools.partial(kernel, n, sub),
            out_shape=jax.ShapeDtypeStruct(x.shape, BF16),
            in_specs=[pl.BlockSpec(memory_space=pl.ANY)] * 3,
            out_specs=pl.BlockSpec(memory_space=pl.ANY),
            scratch_shapes=[
                buffer, buffer, buffer, buffer, temp, temp, far_w, far_w, near_w, near_w,
                pltpu.VMEM((2, far, chips, per // sub, rows, 2 * rows), BF16),
                pltpu.VMEM((2, chips, per, 2, rows, rows), BF16),
                dma((chunks,)), dma((chunks,)), dma((chunks,)), dma((chunks,)),
                dma((chunks,)), dma((chunks,)), dma((chunks,)), dma((chunks,)),
                dma((2, chunks)), dma((2, chunks)),
                dma((2,)), dma((2,)), dma((2, sub)), dma((2, sub)),
                dma((2,)),
            ],
            compiler_params=pltpu.CompilerParams(
                collective_id=0, has_side_effects=True, vmem_limit_bytes=62 * 2 ** 20),
        )(x, w_first.reshape(by_chip), w_second.reshape(by_chip))
        return result.reshape(signal.shape)

    row_spec = P(("dp", "sp"), None)
    weight_spec = P(None, "sp", None, None, None)
    return jax.shard_map(device_program, mesh=mesh, in_specs=(row_spec, weight_spec, weight_spec), out_specs=row_spec, check_vma=False)
```

time: 1740 us -> 607 us (0.35)
  waiting for transfers between devices: 1300 us -> 0 us
  Pallas kernels: 0 us -> 601 us
  matrix products: 273 us -> 0 us
  local copies, waits for them, and re-layouts: 139 us -> 5.89 us
  starting transfers between devices: 20.1 us -> 0 us
    ppermute x8 -> x0, waiting for transfers between devices: 1300 us -> none  [apply_map(): partner = lax.ppermute(act_blocks, 'sp', pairing)]
    pallas_call x0 -> x1, Pallas kernels: none -> 601 us  [device_program(): pl.pallas_call(functools.partial(kernel, n, sub), out_shape=jax.ShapeDtyp...]
    dot_general x40 -> x0, matrix products: 273 us -> none  [the longest x20 175 us: mix_blocks(): jnp.einsum('lij,ljc->lic', weights[:, 1], partner, preferred_element_type...]
    rev x12 -> x0, local copies, waits for them, and re-layouts: 74.3 us -> none  [local_partner(): return grouped[:, ::-1].reshape(act_blocks.shape)]
    slice x2 -> x0, local copies, waits for them, and re-layouts: 30.1 us -> none  [apply_map(): act_blocks = mix_blocks(act_blocks, partner, weights[stage])]
    ppermute x8 -> x0, starting transfers between devices: 20.1 us -> none  [apply_map(): partner = lax.ppermute(act_blocks, 'sp', pairing)]
  transfers between devices with their start and end apart: 8 -> 0, of which waited for: 7 -> 0; matrix products, arithmetic and copies ran while one was open for 6% -> 0% of each run, Pallas kernels for 0% -> 0%
where the time goes in v2:
time: 607 us
  Pallas kernels  601 us (99%)
    pallas_call x1, Pallas kernels, device_program(): pl.pallas_call(functools.partial(kernel, n, sub), out_shape=jax.ShapeDtyp...  601 us

profile of v2, /device:TPU:84, one launch (start us, length us, event | category | flops | bytes accessed | tf_op | source)
XLA Modules:
  0.0 606.5 jit_solution(6460175051089433517)
XLA Ops:
  0.0 600.6 %shard_map.37 = bf16[64,64,768]{2,1,0:T(8,128)(2,1)} custom-call(bf16[64,64,768]{2,1,0:T(8,128)(2,1)} %bitcast.7, bf16[10,8,8,2,64,64]{5,4,3,2,1,0:T(8,128)(2,1)} %bitcast.5, bf16[10,8,8,2,64,64]{5,4,3,2,1,0:T(8,128)(2,1)} %bitcast.6), custom_call_target="tpu_custom_call" | custom-call | tf_op jit(solution)/shard_map/pallas_call | solution.py:328
  600.7 5.9 copy.5

commit v3 on v2

--- a/solution.py
+++ b/solution.py
@@ -290,7 +290,7 @@
                 send_sem=o2_snd.at[c], recv_sem=o2_rcv.at[c],
                 device_id=on(z), device_id_type=MESH).start()
 
-        pltpu.make_async_copy(r3.at[c, of(chip)], out.at[of(chip), :, cols(c)], o2_rcv.at[c]).start()
+        out[of(chip), :, cols(c)] = r3[c, of(chip)]
 
     for m in range(2):
         wait_for(t_of[m].at[:, pl.ds(0, chips - 1), mine_l], z_snd.at[m])
@@ -302,7 +302,7 @@
         wait_for(others(r1, c), x_snd.at[c])
         wait_for(others(r2, c), i2_snd.at[c])
         wait_for(others(r3, c), o2_snd.at[c])
-        wait_for(out.at[:, :, cols(c)], o2_rcv.at[c])
+        wait_for(out.at[pl.ds(0, (chips - 1) * per), :, cols(c)], o2_rcv.at[c])
 
 
 def solution(mesh):
@@ -327,9 +327,9 @@
         near_w = pltpu.VMEM((near, blocks, rows, 2 * rows), BF16)
         result = pl.pallas_call(
             functools.partial(kernel, n, sub),
-            out_shape=jax.ShapeDtypeStruct(x.shape, BF16),
+            out_shape=pltpu.VMEM(x.shape, BF16),
             in_specs=[pl.BlockSpec(memory_space=pl.ANY)] * 3,
-            out_specs=pl.BlockSpec(memory_space=pl.ANY),
+            out_specs=pl.BlockSpec(memory_space=pltpu.VMEM),
             scratch_shapes=[
                 buffer, buffer, buffer, buffer, temp, temp, far_w, far_w, near_w, near_w,
                 pltpu.VMEM((2, far, chips, per // sub, rows, 2 * rows), BF16),
@@ -341,7 +341,7 @@
                 dma((2,)),
             ],
             compiler_params=pltpu.CompilerParams(
-                collective_id=0, has_side_effects=True, vmem_limit_bytes=62 * 2 ** 20),
+                collective_id=0, has_side_effects=True, vmem_limit_bytes=56 * 2 ** 20),
         )(x, w_first.reshape(by_chip), w_second.reshape(by_chip))
         return result.reshape(signal.shape)
 

time: 607 us -> 604 us (level)
  no operation moved by 1% of the time
where the time goes in v3:
time: 604 us; the launch traced here: 603 us
  Pallas kernels  601 us (100%)
    pallas_call x1, Pallas kernels, device_program(): pl.pallas_call(functools.partial(kernel, n, sub), out_shape=pltpu.VMEM(x....  601 us

profile of v3, /device:TPU:84, one launch (start us, length us, event | category | flops | bytes accessed | tf_op | source)
XLA Modules:
  0.0 603.4 jit_solution(13939100976994170548)
XLA Ops:
  0.0 600.6 %shard_map.37 = bf16[64,64,768]{2,1,0:T(8,128)(2,1)S(1)} custom-call(bf16[64,64,768]{2,1,0:T(8,128)(2,1)} %bitcast.7, bf16[10,8,8,2,64,64]{5,4,3,2,1,0:T(8,128)(2,1)} %bitcast.5, bf16[10,8,8,2,64,64]{5,4,3,2,1,0:T(8,128)(2,1)} %bitcast.6), custom_call_target="tpu_custom_call" | custom-call | tf_op jit(solution)/shard_map/pallas_call | solution.py:328
  600.7 2.7 copy.5

commit v4 on v3

--- a/solution.py
+++ b/solution.py
@@ -71,8 +71,13 @@
     mine_l = pl.ds(part * take, take)
 
     def peer(t):
-        side = 1 - 2 * (t % 2)
-        return (chip + chips // 2 + side * ((t + 1) // 2) + chips) % chips
+        if chips == 2:
+            return (chip + 1) % chips
+        pair, last = t // 2, t // (chips - 2)
+        reach = chips // 2 - 1
+        distance = (reach - pair) + core * (2 * pair + 1 - reach)
+        offset = distance + (t % 2) * (chips - 2 * distance)
+        return (chip + last * (chips // 2) + (1 - last) * offset) % chips
 
     def on(z):
         return {"sp": z * CORES + core}

time: 604 us -> 596 us (0.987)
  Pallas kernels: 601 us -> 589 us
    pallas_call x1, Pallas kernels: 601 us -> 589 us  [device_program(): pl.pallas_call(functools.partial(kernel, n, sub), out_shape=pltpu.VMEM(x....]
where the time goes in v4:
time: 596 us; the launch traced here: 592 us
  Pallas kernels  589 us (99%)
    pallas_call x1, Pallas kernels, device_program(): pl.pallas_call(functools.partial(kernel, n, sub), out_shape=pltpu.VMEM(x....  589 us

profile of v4, /device:TPU:84, one launch (start us, length us, event | category | flops | bytes accessed | tf_op | source)
XLA Modules:
  0.0 591.8 jit_solution(7093399390957585525)
XLA Ops:
  0.0 589.1 %shard_map.37 = bf16[64,64,768]{2,1,0:T(8,128)(2,1)S(1)} custom-call(bf16[64,64,768]{2,1,0:T(8,128)(2,1)} %bitcast.7, bf16[10,8,8,2,64,64]{5,4,3,2,1,0:T(8,128)(2,1)} %bitcast.5, bf16[10,8,8,2,64,64]{5,4,3,2,1,0:T(8,128)(2,1)} %bitcast.6), custom_call_target="tpu_custom_call" | custom-call | tf_op jit(solution)/shard_map/pallas_call | solution.py:333
  589.1 2.7 copy.5

commit v5 on v4

--- a/solution.py
+++ b/solution.py
@@ -202,13 +202,13 @@
     send_signal(0)
     run_jobs(0, far)
     send_weights(0)
-
-    @pl.loop(1, chunks)
-    def _(c):
-        send_signal(c)
-
     run_jobs(far, 2 * far)
     send_weights(1)
+
+    @pl.loop(1, chunks)
+    def _(c):
+        send_signal(c)
+
     run_jobs(2 * far, len(jobs))
     start_gather(0)
     wait_gather(0)

time: 596 us -> 596 us (level)
  no operation moved by 1% of the time
where the time goes in v5:
time: 596 us; the launch traced here: 592 us
  Pallas kernels  590 us (99%)
    pallas_call x1, Pallas kernels, device_program(): pl.pallas_call(functools.partial(kernel, n, sub), out_shape=pltpu.VMEM(x....  590 us

profile of v5, /device:TPU:84, one launch (start us, length us, event | category | flops | bytes accessed | tf_op | source)
XLA Modules:
  0.0 592.4 jit_solution(12046064521309499492)
XLA Ops:
  0.0 589.6 %shard_map.37 = bf16[64,64,768]{2,1,0:T(8,128)(2,1)S(1)} custom-call(bf16[64,64,768]{2,1,0:T(8,128)(2,1)} %bitcast.7, bf16[10,8,8,2,64,64]{5,4,3,2,1,0:T(8,128)(2,1)} %bitcast.5, bf16[10,8,8,2,64,64]{5,4,3,2,1,0:T(8,128)(2,1)} %bitcast.6), custom_call_target="tpu_custom_call" | custom-call | tf_op jit(solution)/shard_map/pallas_call | solution.py:333
  589.7 2.7 copy.5
